TPU v7x, 256 devices: a whole 4x4x8 slice. The times are simulated.
256 devices in a mesh: dop: 32 (over z, y), slow: 8 (over x, core).
Axes of the slice: x: 4, y: 4, z: 8, core: 2. Of those that a mesh axis runs over, the one named last changes fastest.
Arguments:
- profiles: bfloat16 [64, 2, 1024, 2048], P('slow', None, 'dop'), may hold values from -6 to 6
- range_walk: int32 [2048], replicated, may hold values from -32 to 32
- band_order: int32 [256], replicated, may hold values from 0 to 255, each once
Outputs:
- ambiguity: float32 [2048, 1024], P(('dop', 'slow'))
Inputs may be any that keep to these rules, and one draw needn't show every extreme that they name: `band_order`: each band number appears exactly once.
All inputs are finite; a program needn't handle non-finite values.
Results may differ from a plain program's by a relative error of at most 0.00067.
Values sent between devices are 32-bit elements; how exact they have to be, the bound alone decides.
No kernel may reach another device: no remote copies, remote signals or barrier semaphores. Data moves between devices by JAX's collectives and lax.ppermute only.
A program may use at most 64 MiB of HBM per device.

v0:
```python
import math
import jax
import jax.numpy as jnp
from jax import lax
from jax.sharding import PartitionSpec as P

WALK = 32


def from_behind(value, axis, steps):
    count = lax.axis_size(axis)
    leading, last = (max(0, -steps), min(count, count - steps))
    return lax.ppermute(value, axis, [(source, source + steps) for source in range(leading, last)])


def cut_along(x, dim, devices):
    before, after = (x.shape[:dim], x.shape[dim + 1 :])
    return jnp.moveaxis(x.reshape(*before, devices, -1, *after), dim, 0)


def summed_on_arrival(x, axis, dim):
    tiles = cut_along(x, dim, lax.axis_size(axis))
    arrived = lax.all_to_all(tiles, axis, split_axis=0, concat_axis=0, tiled=True)
    return arrived.sum(axis=0)


def fourier_tables(length):
    counter = jnp.arange(length, dtype=jnp.int32)
    phases = counter[:, None] * counter[None, :] % length
    angles = phases.astype(jnp.float32) * (2.0 * math.pi / length)
    return (jnp.cos(angles).astype(jnp.bfloat16), jnp.sin(angles).astype(jnp.bfloat16))


def batch_powers(block, cosine, sine_table):
    count = block.shape[0]
    delays = block.shape[2]
    bins = block.shape[3]
    stacked = block.reshape(count * 2 * delays, bins)
    first = jnp.dot(stacked, cosine, preferred_element_type=jnp.float32).reshape(
        count, 2, delays, bins
    )
    second = jnp.dot(stacked, sine_table, preferred_element_type=jnp.float32).reshape(
        count, 2, delays, bins
    )
    real_part = first[:, 0] + second[:, 1]
    imag_part = first[:, 1] - second[:, 0]
    return real_part * real_part + imag_part * imag_part


def walk_align(padded, offsets, out_rows, reach):
    moves = offsets + reach
    levels = max(1, (2 * reach).bit_length())
    needed = out_rows + (1 << levels) - 1
    current = jnp.pad(padded, ((0, 0), (0, needed - padded.shape[1]), (0, 0)))
    for level in range(levels):
        stride = 1 << level
        taken = (moves // stride % 2 == 1)[:, None, :]
        current = jnp.where(taken, current[:, stride:], current[:, :-stride])
    return current


def permute_bands(values, band_order, band_count):
    picker = (band_order[:, None] == jnp.arange(band_count, dtype=jnp.int32)[None, :]).astype(
        jnp.float32
    )
    return jnp.einsum("bc,...cj->...bj", picker, values, precision=lax.Precision.HIGHEST)


def on_device(profiles, range_walk, band_order):
    batch_count = profiles.shape[0]
    local_rows = profiles.shape[2]
    doppler_bins = profiles.shape[3]
    dop_count = lax.axis_size("dop")
    slow_count = lax.axis_size("slow")
    total_batches = batch_count * slow_count
    band_count = dop_count * slow_count
    band_rows = doppler_bins // band_count
    scale = 1.0 / (total_batches * doppler_bins)
    cosine, sine_table = fourier_tables(doppler_bins)
    powers = batch_powers(profiles, cosine, sine_table)
    batches = lax.axis_index("slow") * batch_count + jnp.arange(batch_count, dtype=jnp.int32)
    offsets = range_walk[None, :] * batches[:, None] // total_batches
    widened = jnp.pad(powers, ((0, 0), (2 * WALK, 2 * WALK), (0, 0)))
    gathered = jnp.sum(walk_align(widened, offsets, local_rows + 2 * WALK, WALK), axis=0)
    lower_rim = gathered[:WALK]
    upper_rim = gathered[local_rows + WALK :]
    own_rows = gathered[WALK : local_rows + WALK]
    from_below = from_behind(upper_rim, "dop", 1)
    from_above = from_behind(lower_rim, "dop", -1)
    own_rows = own_rows.at[:WALK].add(from_below)
    own_rows = own_rows.at[local_rows - WALK :].add(from_above)
    partial_value = own_rows * scale
    ordered = permute_bands(
        partial_value.reshape(local_rows, band_count, band_rows), band_order, band_count
    )
    grouped = ordered.reshape(local_rows, dop_count, slow_count, band_rows).transpose(0, 2, 1, 3)
    grouped = grouped.reshape(local_rows, doppler_bins)
    summed = summed_on_arrival(grouped, "slow", 1)
    result = lax.all_to_all(summed, "dop", split_axis=1, concat_axis=0, tiled=True)
    return result.T


def solution(mesh):
    placed = (P("slow", None, "dop", None), P(), P())
    return jax.shard_map(
        on_device, mesh=mesh, in_specs=placed, out_specs=P(("dop", "slow"), None), check_vma=False
    )
```

profile of v0, /device:TPU:1, one launch (start us, length us, event | category | flops | bytes accessed | tf_op | source)
XLA Modules:
  0.0 232.3 jit_solution(15600399316770278802)
XLA Ops:
  0.0 1.6 copy-done
  1.6 63.9 %fusion.7 = f32[2048,512]{0,1:T(8,128)} fusion(bf16[512,2048]{1,0:T(8,128)(2,1)S(1)} %bitcast.66), kind=kOutput, calls=%fused_computation.19 | convolution fusion | flops 4357881856 | bytes 6291456 | tf_op jit(solution)/shard_map/dot_general | solution.py:39
  65.5 64.4 %fusion.8 = f32[2048,512]{0,1:T(8,128)} fusion(bf16[512,2048]{1,0:T(8,128)(2,1)S(1)} %bitcast.65), kind=kOutput, calls=%fused_computation.20 | convolution fusion | flops 4357881856 | bytes 6291456 | tf_op jit(solution)/shard_map/dot_general | solution.py:42
  130.4 4.5 %fusion.15 = f32[8,32,2048]{2,1,0:T(8,128)S(1)} fusion(f32[8,2,32,2048]{3,2,1,0:T(8,128)} %bitcast.71, f32[8,2,32,2048]{3,2,1,0:T(8,128)} %bitcast.70), kind=kLoop, calls=%fused_computation.27 | loop fusion | flops 2621440 | bytes 10485760 | tf_op jit(solution)/shard_map/add | solution.py:47
  134.9 7.2 %fusion.6 = f32[8,222,2048]{2,1,0:T(8,128)} fusion(f32[8,32,2048]{2,1,0:T(8,128)S(1)} %fusion.15, pred[8,2048]{1,0:T(8,128)(4,1)S(1)} %get-tuple-element.51), kind=kLoop, calls=%fused_computation.13 | loop fusion | flops 3637248 | bytes 16662528 | tf_op jit(solution)/shard_map/jit(_where)/select_n | solution.py:58
  142.1 10.7 %slice_select_fusion = f32[8,220,2048]{2,1,0:T(8,128)S(1)} fusion(f32[8,222,2048]{2,1,0:T(8,128)} %fusion.6, pred[8,2048]{1,0:T(8,128)(4,1)S(1)} %get-tuple-element.53), kind=kLoop, calls=%fused_computation.14 | loop fusion | flops 3604480 | bytes 43270144 | tf_op jit(solution)/shard_map/jit(_where)/select_n | solution.py:58
  152.8 3.4 %slice_select_fusion.1 = f32[8,216,2048]{2,1,0:T(8,128)S(1)} fusion(f32[8,220,2048]{2,1,0:T(8,128)S(1)} %slice_select_fusion, pred[8,2048]{1,0:T(8,128)(4,1)S(1)} %get-tuple-element.49), kind=kLoop, calls=%fused_computation.15 | loop fusion | flops 3538944 | bytes 42483712 | tf_op jit(solution)/shard_map/jit(_where)/select_n | solution.py:58
  156.2 6.7 %slice_select_fusion.2 = f32[8,208,2048]{2,1,0:T(8,128)} fusion(f32[8,216,2048]{2,1,0:T(8,128)S(1)} %slice_select_fusion.1, pred[8,2048]{1,0:T(8,128)(4,1)S(1)} %get-tuple-element.52), kind=kLoop, calls=%fused_computation.16 | loop fusion | flops 3407872 | bytes 40910848 | tf_op jit(solution)/shard_map/jit(_where)/select_n | solution.py:58
  162.9 9.4 %slice_select_fusion.3 = f32[8,192,2048]{2,1,0:T(8,128)S(1)} fusion(f32[8,208,2048]{2,1,0:T(8,128)} %slice_select_fusion.2, pred[8,2048]{1,0:T(8,128)(4,1)S(1)} %get-tuple-element.50), kind=kLoop, calls=%fused_computation.17 | loop fusion | flops 3145728 | bytes 37765120 | tf_op jit(solution)/shard_map/jit(_where)/select_n | solution.py:58
  172.3 3.7 %slice_select_fusion.4 = f32[8,160,2048]{2,1,0:T(8,128)S(1)} fusion(f32[8,192,2048]{2,1,0:T(8,128)S(1)} %slice_select_fusion.3, pred[8,2048]{1,0:T(8,128)(4,1)S(1)} %get-tuple-element.48), kind=kLoop, calls=%fused_computation.18 | loop fusion | flops 2621440 | bytes 31473664 | tf_op jit(solution)/shard_map/jit(_where)/select_n | solution.py:58
  176.0 1.2 fusion.11
  177.3 4.0 %collective-permute-start = (f32[32,2048]{1,0:T(8,128)S(1)}, f32[32,2048]{1,0:T(8,128)S(1)}, u32[]{:S(2)}, u32[]{:S(2)}) collective-permute-start(f32[32,2048]{1,0:T(8,128)S(1)} %get-tuple-element.45), channel_id=1, source_target_pairs={{0,8},{8,16},{16,24},{24,32},{32,40},{40,48},{48,56},{56,64},{64,7... | collective-permute-start | bytes 786440 | tf_op jit(solution)/shard_map/ppermute | solution.py:13
  181.4 1.3 collective-permute-start.1
  182.7 3.7 %collective-permute-done = f32[32,2048]{1,0:T(8,128)S(1)} collective-permute-done((f32[32,2048]{1,0:T(8,128)S(1)}, f32[32,2048]{1,0:T(8,128)S(1)}, u32[]{:S(2)}, u32[]{:S(2)}) %collective-permute-start) | collective-permute-done | bytes 262176 | tf_op jit(solution)/shard_map/ppermute | solution.py:13
  186.3 3.8 %collective-permute-done.1 = f32[32,2048]{1,0:T(8,128)S(1)} collective-permute-done((f32[32,2048]{1,0:T(8,128)S(1)}, f32[32,2048]{1,0:T(8,128)S(1)}, u32[]{:S(2)}, u32[]{:S(2)}) %collective-permute-start.1) | collective-permute-done | bytes 262176 | tf_op jit(solution)/shard_map/ppermute | solution.py:13
  191.0 1.1 convolution_bitcast_fusion
  192.1 1.4 copy.27
  193.4 1.1 copy.37
  194.5 1.5 copy.29
  196.0 12.4 %all_to_all.24 = f32[8,32,256]{2,1,0:T(8,128)S(1)} all-to-all(f32[8,32,256]{2,1,0:T(8,128)S(1)} %copy.29), channel_id=1, replica_groups=mesh['dop'=32,'slow'=8] {'slow'}, dimensions={0} | all-to-all | bytes 524288 | tf_op jit(solution)/shard_map/all_to_all | solution.py:23
  208.7 21.5 %all_to_all.25 = f32[32,1,256]{2,1,0:T(1,128)S(1)} all-to-all(f32[32,1,256]{2,1,0:T(1,128)S(1)} %reshape.392), channel_id=1, replica_groups=mesh['dop'=32,'slow'=8] {'dop'}, dimensions={0} | all-to-all | bytes 65536 | tf_op jit(solution)/shard_map/all_to_all | solution.py:99
  230.2 0.5 broadcast.746
  230.7 0.7 reduce.6
  231.6 0.7 all_to_all.21
  (20 shorter events, 1.7 us)
Async XLA Ops:
  0.0 1.6 copy-start
  65.5 64.4 %copy-start.2 = (s32[2048]{0:T(1024)S(1)}, s32[2048]{0:T(1024)}, u32[]{:S(2)}) copy-start(s32[2048]{0:T(1024)} %param.12) | copy-start | bytes 24580
  176.0 14.9 %copy-start.3 = (s32[256]{0:T(256)S(1)}, s32[256]{0:T(256)}, u32[]{:S(2)}) copy-start(s32[256]{0:T(256)} %param.13) | copy-start | bytes 3076
  176.0 56.3 %copy-start.1 = (bf16[8,2,32,2048]{3,2,1,0:T(8,128)(2,1)S(1)}, bf16[8,2,32,2048]{3,2,1,0:T(8,128)(2,1)}, u32[]{:S(2)}) copy-start(bf16[8,2,32,2048]{3,2,1,0:T(8,128)(2,1)} %param.11) | copy-start | bytes 6291460
  177.3 9.0 %collective-permute-start = (f32[32,2048]{1,0:T(8,128)S(1)}, f32[32,2048]{1,0:T(8,128)S(1)}, u32[]{:S(2)}, u32[]{:S(2)}) collective-permute-start(f32[32,2048]{1,0:T(8,128)S(1)} %get-tuple-element.45), channel_id=1, source_target_pairs={{0,8},{8,16},{16,24},{24,32},{32,40},{40,48},{48,56},{56,64},{64,7... | collective-permute-start | bytes 786440 | tf_op jit(solution)/shard_map/ppermute | solution.py:13
  181.4 8.8 %collective-permute-start.1 = (f32[32,2048]{1,0:T(8,128)S(1)}, f32[32,2048]{1,0:T(8,128)S(1)}, u32[]{:S(2)}, u32[]{:S(2)}) collective-permute-start(f32[32,2048]{1,0:T(8,128)S(1)} %get-tuple-element.46), channel_id=1, source_target_pairs={{8,0},{16,8},{24,16},{32,24},{40,32},{48,40},{56,48},{64,56},{72,6... | collective-permute-start | bytes 786440 | tf_op jit(solution)/shard_map/ppermute | solution.py:13
where the time goes:
time: 233 us; the launch traced here: 232 us
  matrix products  129 us (55%)
  other arithmetic  48.1 us (21%)
  blocking collectives  33.9 us (15%)
  local copies, waits for them, and re-layouts  7.89 us (3%)
  waiting for transfers between devices  7.5 us (3%)
  starting transfers between devices  5.33 us (2%)
    dot_general x1, matrix products, batch_powers(): jnp.dot(stacked, sine_table, preferred_element_type=jnp.float32)  64.4 us
    dot_general x1, matrix products, batch_powers(): jnp.dot(stacked, cosine, preferred_element_type=jnp.float32)  63.9 us
    select_n x6, other arithmetic, walk_align(): current = jnp.where(taken, current[:, stride:], current[:, :-stride])  41 us
    all_to_all x1, blocking collectives, on_device(): lax.all_to_all(summed, 'dop', split_axis=1, concat_axis=0, tiled=True)  21.5 us
    all_to_all x1, blocking collectives, summed_on_arrival(): lax.all_to_all(tiles, axis, split_axis=0, concat_axis=0, tiled=True)  12.4 us
    ppermute x2, waiting for transfers between devices, from_behind(): lax.ppermute(value, axis, [(source, source + steps) for source in range(l...  7.5 us
    ppermute x2, starting transfers between devices, from_behind(): lax.ppermute(value, axis, [(source, source + steps) for source in range(l...  5.33 us
  transfers between devices with their start and end apart: 2, of which 2 were waited for; matrix products, arithmetic and copies ran while one was open for 0% of the time, Pallas kernels for 0%

commit v1 on v0

--- a/solution.py
+++ b/solution.py
@@ -96,7 +96,10 @@
     grouped = ordered.reshape(local_rows, dop_count, slow_count, band_rows).transpose(0, 2, 1, 3)
     grouped = grouped.reshape(local_rows, doppler_bins)
     summed = summed_on_arrival(grouped, "slow", 1)
-    result = lax.all_to_all(summed, "dop", split_axis=1, concat_axis=0, tiled=True)
+    result = jnp.concatenate(
+        lax.all_to_all(jnp.stack(jnp.split(summed, lax.axis_size("dop"), axis=1)), "dop", 0, 0),
+        axis=0,
+    )
     return result.T
 
 

time: 233 us -> 235 us (level)
  no operation moved by 1% of the time
where the time goes in v1:
time: 235 us
  matrix products  129 us (55%)
  other arithmetic  48 us (20%)
  blocking collectives  33.9 us (14%)
  local copies, waits for them, and re-layouts  10.2 us (4%)
  waiting for transfers between devices  7.5 us (3%)
  starting transfers between devices  5.33 us (2%)
    dot_general x1, matrix products, batch_powers(): jnp.dot(stacked, sine_table, preferred_element_type=jnp.float32)  64.5 us
    dot_general x1, matrix products, batch_powers(): jnp.dot(stacked, cosine, preferred_element_type=jnp.float32)  63.9 us
    select_n x6, other arithmetic, walk_align(): current = jnp.where(taken, current[:, stride:], current[:, :-stride])  41 us
    all_to_all x1, blocking collectives, on_device(): lax.all_to_all(jnp.stack(jnp.split(summed, lax.axis_size('dop'), axis=1))...  21.5 us
    all_to_all x1, blocking collectives, summed_on_arrival(): lax.all_to_all(tiles, axis, split_axis=0, concat_axis=0, tiled=True)  12.4 us
    ppermute x2, waiting for transfers between devices, from_behind(): lax.ppermute(value, axis, [(source, source + steps) for source in range(l...  7.5 us
    ppermute x2, starting transfers between devices, from_behind(): lax.ppermute(value, axis, [(source, source + steps) for source in range(l...  5.33 us
  transfers between devices with their start and end apart: 2, of which 2 were waited for; matrix products, arithmetic and copies ran while one was open for 0% of the time, Pallas kernels for 0%

profile of v1, /device:TPU:1, one launch (start us, length us, event | category | flops | bytes accessed | tf_op | source)
XLA Modules:
  0.0 235.0 jit_solution(1564560835677232557)
XLA Ops:
  0.0 1.6 copy-done
  1.6 63.9 %fusion.7 = f32[2048,512]{0,1:T(8,128)} fusion(bf16[512,2048]{1,0:T(8,128)(2,1)S(1)} %bitcast.124), kind=kOutput, calls=%fused_computation.19 | convolution fusion | flops 4357881856 | bytes 6291456 | tf_op jit(solution)/shard_map/dot_general | solution.py:39
  65.5 64.5 %fusion.8 = f32[2048,512]{0,1:T(8,128)} fusion(bf16[512,2048]{1,0:T(8,128)(2,1)S(1)} %bitcast.123), kind=kOutput, calls=%fused_computation.20 | convolution fusion | flops 4357881856 | bytes 6291456 | tf_op jit(solution)/shard_map/dot_general | solution.py:42
  130.5 4.5 %fusion.15 = f32[8,32,2048]{2,1,0:T(8,128)S(1)} fusion(f32[8,2,32,2048]{3,2,1,0:T(8,128)} %bitcast.129, f32[8,2,32,2048]{3,2,1,0:T(8,128)} %bitcast.128), kind=kLoop, calls=%fused_computation.27 | loop fusion | flops 2621440 | bytes 10485760 | tf_op jit(solution)/shard_map/add | solution.py:47
  135.0 7.2 %fusion.6 = f32[8,222,2048]{2,1,0:T(8,128)} fusion(f32[8,32,2048]{2,1,0:T(8,128)S(1)} %fusion.15, pred[8,2048]{1,0:T(8,128)(4,1)S(1)} %get-tuple-element.83), kind=kLoop, calls=%fused_computation.13 | loop fusion | flops 3637248 | bytes 16662528 | tf_op jit(solution)/shard_map/jit(_where)/select_n | solution.py:58
  142.2 10.7 %slice_select_fusion = f32[8,220,2048]{2,1,0:T(8,128)S(1)} fusion(f32[8,222,2048]{2,1,0:T(8,128)} %fusion.6, pred[8,2048]{1,0:T(8,128)(4,1)S(1)} %get-tuple-element.85), kind=kLoop, calls=%fused_computation.14 | loop fusion | flops 3604480 | bytes 43270144 | tf_op jit(solution)/shard_map/jit(_where)/select_n | solution.py:58
  152.9 3.4 %slice_select_fusion.1 = f32[8,216,2048]{2,1,0:T(8,128)S(1)} fusion(f32[8,220,2048]{2,1,0:T(8,128)S(1)} %slice_select_fusion, pred[8,2048]{1,0:T(8,128)(4,1)S(1)} %get-tuple-element.81), kind=kLoop, calls=%fused_computation.15 | loop fusion | flops 3538944 | bytes 42483712 | tf_op jit(solution)/shard_map/jit(_where)/select_n | solution.py:58
  156.2 6.7 %slice_select_fusion.2 = f32[8,208,2048]{2,1,0:T(8,128)} fusion(f32[8,216,2048]{2,1,0:T(8,128)S(1)} %slice_select_fusion.1, pred[8,2048]{1,0:T(8,128)(4,1)S(1)} %get-tuple-element.84), kind=kLoop, calls=%fused_computation.16 | loop fusion | flops 3407872 | bytes 40910848 | tf_op jit(solution)/shard_map/jit(_where)/select_n | solution.py:58
  162.9 9.4 %slice_select_fusion.3 = f32[8,192,2048]{2,1,0:T(8,128)S(1)} fusion(f32[8,208,2048]{2,1,0:T(8,128)} %slice_select_fusion.2, pred[8,2048]{1,0:T(8,128)(4,1)S(1)} %get-tuple-element.82), kind=kLoop, calls=%fused_computation.17 | loop fusion | flops 3145728 | bytes 37765120 | tf_op jit(solution)/shard_map/jit(_where)/select_n | solution.py:58
  172.3 3.7 %slice_select_fusion.4 = f32[8,160,2048]{2,1,0:T(8,128)S(1)} fusion(f32[8,192,2048]{2,1,0:T(8,128)S(1)} %slice_select_fusion.3, pred[8,2048]{1,0:T(8,128)(4,1)S(1)} %get-tuple-element.80), kind=kLoop, calls=%fused_computation.18 | loop fusion | flops 2621440 | bytes 31473664 | tf_op jit(solution)/shard_map/jit(_where)/select_n | solution.py:58
  176.0 1.2 fusion.11
  177.3 4.0 %collective-permute-start = (f32[32,2048]{1,0:T(8,128)S(1)}, f32[32,2048]{1,0:T(8,128)S(1)}, u32[]{:S(2)}, u32[]{:S(2)}) collective-permute-start(f32[32,2048]{1,0:T(8,128)S(1)} %get-tuple-element.45), channel_id=1, source_target_pairs={{0,8},{8,16},{16,24},{24,32},{32,40},{40,48},{48,56},{56,64},{64,7... | collective-permute-start | bytes 786440 | tf_op jit(solution)/shard_map/ppermute | solution.py:13
  181.4 1.3 collective-permute-start.1
  182.7 3.7 %collective-permute-done = f32[32,2048]{1,0:T(8,128)S(1)} collective-permute-done((f32[32,2048]{1,0:T(8,128)S(1)}, f32[32,2048]{1,0:T(8,128)S(1)}, u32[]{:S(2)}, u32[]{:S(2)}) %collective-permute-start) | collective-permute-done | bytes 262176 | tf_op jit(solution)/shard_map/ppermute | solution.py:13
  186.3 3.8 %collective-permute-done.1 = f32[32,2048]{1,0:T(8,128)S(1)} collective-permute-done((f32[32,2048]{1,0:T(8,128)S(1)}, f32[32,2048]{1,0:T(8,128)S(1)}, u32[]{:S(2)}, u32[]{:S(2)}) %collective-permute-start.1) | collective-permute-done | bytes 262176 | tf_op jit(solution)/shard_map/ppermute | solution.py:13
  191.0 1.1 convolution_bitcast_fusion
  192.1 1.4 copy.105
  193.4 1.0 copy.146
  194.5 1.5 copy.107
  196.0 12.4 %all_to_all.10 = f32[8,32,256]{2,1,0:T(8,128)S(1)} all-to-all(f32[8,32,256]{2,1,0:T(8,128)S(1)} %copy.107), channel_id=1, replica_groups=mesh['dop'=32,'slow'=8] {'slow'}, dimensions={0} | all-to-all | bytes 524288 | tf_op jit(solution)/shard_map/all_to_all | solution.py:23
  211.3 21.5 %all_to_all.11 = f32[32,1,256]{2,1,0:T(1,128)S(1)} all-to-all(f32[32,1,256]{2,1,0:T(1,128)S(1)} %reshape.393), channel_id=1, replica_groups=mesh['dop'=32,'slow'=8] {'dop'}, dimensions={0} | all-to-all | bytes 65536 | tf_op jit(solution)/shard_map/all_to_all | solution.py:100
  232.9 0.5 broadcast.746
  233.4 0.7 reduce.6
  234.2 0.7 reshape.391
  (83 shorter events, 4.0 us)
Async XLA Ops:
  0.0 1.6 copy-start
  65.5 64.5 %copy-start.2 = (s32[2048]{0:T(1024)S(1)}, s32[2048]{0:T(1024)}, u32[]{:S(2)}) copy-start(s32[2048]{0:T(1024)} %param.12) | copy-start | bytes 24580
  176.0 14.9 %copy-start.3 = (s32[256]{0:T(256)S(1)}, s32[256]{0:T(256)}, u32[]{:S(2)}) copy-start(s32[256]{0:T(256)} %param.13) | copy-start | bytes 3076
  176.0 58.9 %copy-start.1 = (bf16[8,2,32,2048]{3,2,1,0:T(8,128)(2,1)S(1)}, bf16[8,2,32,2048]{3,2,1,0:T(8,128)(2,1)}, u32[]{:S(2)}) copy-start(bf16[8,2,32,2048]{3,2,1,0:T(8,128)(2,1)} %param.11) | copy-start | bytes 6291460
  177.3 9.0 %collective-permute-start = (f32[32,2048]{1,0:T(8,128)S(1)}, f32[32,2048]{1,0:T(8,128)S(1)}, u32[]{:S(2)}, u32[]{:S(2)}) collective-permute-start(f32[32,2048]{1,0:T(8,128)S(1)} %get-tuple-element.45), channel_id=1, source_target_pairs={{0,8},{8,16},{16,24},{24,32},{32,40},{40,48},{48,56},{56,64},{64,7... | collective-permute-start | bytes 786440 | tf_op jit(solution)/shard_map/ppermute | solution.py:13
  181.4 8.8 %collective-permute-start.1 = (f32[32,2048]{1,0:T(8,128)S(1)}, f32[32,2048]{1,0:T(8,128)S(1)}, u32[]{:S(2)}, u32[]{:S(2)}) collective-permute-start(f32[32,2048]{1,0:T(8,128)S(1)} %get-tuple-element.46), channel_id=1, source_target_pairs={{8,0},{16,8},{24,16},{32,24},{40,32},{48,40},{56,48},{64,56},{72,6... | collective-permute-start | bytes 786440 | tf_op jit(solution)/shard_map/ppermute | solution.py:13
